TPU v7x, 512 devices: a whole 4x4x16 slice. The times are simulated.
512 devices in a mesh: seq: 128 (over z, y, core), grp: 4 (over x).
Axes of the slice: x: 4, y: 4, z: 16, core: 2. Of those that a mesh axis runs over, the one named last changes fastest.
Arguments:
- query_nope: bfloat16 [4, 2, 128, 128], P(None, None, 'seq'), may hold values from -12.859821 to 12.859821
- query_rope: bfloat16 [4, 2, 128, 64], P(None, None, 'seq'), may hold values from -150 to 150
- latent_cache: bfloat16 [4, 131072, 576], P(None, ('seq', 'grp')), may hold values from -5 to 5
- lengths: int32 [4], replicated, may hold values from 65536 to 131072
- key_weight: bfloat16 [128, 128, 512], P('seq'), may hold values from -0.5 to 0.5
- value_weight: bfloat16 [128, 512, 128], P('seq'), may hold values from -0.25 to 0.25
- output_weight: bfloat16 [16384, 7168], P('seq', 'grp'), may hold values from -0.1875 to 0.1875
Outputs:
- mixed: bfloat16 [4, 2, 7168], P(None, None, ('grp', 'seq'))
All inputs are finite; a program needn't handle non-finite values.
Results may differ from a plain program's by a relative error of at most 0.0095.
Values may be sent and summed in bfloat16 or wider, within the bound.
A program may use at most 64 MiB of HBM per device.

v0:
```python
import jax
import jax.numpy as jnp
from jax import lax
from jax.sharding import Mesh
from jax.sharding import PartitionSpec as P

SEQ = ("seq_0", "seq_1", "seq_2")
SEQ_GRP = ("seq_0", "seq_1", "seq_2", "grp")
GRP_SEQ = ("grp", "seq_0", "seq_1", "seq_2")


NEGATIVE = -1e30


def from_everyone(array, axis):
    devices = lax.axis_size(axis)
    return lax.all_to_all(
        jnp.broadcast_to(array[None], (devices, *array.shape)), axis, 0, 0, tiled=True
    )


def joined_along(blocks, dim):
    lengths = list(blocks.shape[1:])
    lengths[dim] *= blocks.shape[0]
    return jnp.moveaxis(blocks, 0, dim).reshape(lengths)


def whole_of(array, axes, dim):
    far, near = axes
    blocks = from_everyone(from_everyone(array, far), near)
    return joined_along(blocks.swapaxes(0, 1).reshape(-1, *array.shape), dim)


def collected_together(array, axis):
    leaves = jax.tree.leaves(array)
    sequence = sorted(range(len(leaves)), key=lambda k: -leaves[k].size)
    width = (1, *leaves[sequence[0]].shape)[-1]
    lines = [
        jnp.pad(leaves[k].reshape(-1), (0, -leaves[k].size % width)).reshape(-1, width)
        for k in sequence
    ]
    both, at, found = (from_everyone(jnp.concatenate(lines), axis), 0, {})
    for k, line in zip(sequence, lines):
        slab = both[:, at : at + len(line)].reshape(len(both), -1)
        found[k] = slab[:, : leaves[k].size].reshape(-1, *leaves[k].shape)
        at += len(line)
    numbers = iter(range(len(leaves)))
    return jax.tree.map(lambda _: found[next(numbers)], array)


def folded_in_pairs(pieces, combine):
    while len(jax.tree.leaves(pieces)[0]) > 1:
        pieces = jax.vmap(combine)(
            *(jax.tree.map(lambda part: part[side::2], pieces) for side in (0, 1))
        )
    return jax.tree.map(lambda part: part[0], pieces)


def merged(array, axis, combine):
    pieces = collected_together(array, axis)
    return folded_in_pairs(pieces, combine)


def in_blocks(array, dim, devices):
    before, after = (array.shape[:dim], array.shape[dim + 1 :])
    return jnp.moveaxis(array.reshape(*before, devices, -1, *after), dim, 0)


def sent_and_summed(array, axis, dim):
    devices = lax.axis_size(axis)
    blocks = lax.all_to_all(in_blocks(array, dim, devices), axis, 0, 0, tiled=True)
    return jnp.sum(blocks, axis=0)


def sum_by_axis(array, axes, dim):
    far, near = axes
    blocks = in_blocks(array, dim, lax.axis_size(far))
    nearer = sent_and_summed(blocks, near, dim + 1)
    arrived = lax.all_to_all(nearer, far, split_axis=0, concat_axis=0, tiled=True)
    return arrived.sum(axis=0)


def shard_partial(queries, cache_block, limits, offset, factor, latent_width):
    raw_score = (
        jnp.einsum("bqhd,bpd->bqhp", queries, cache_block, preferred_element_type=jnp.float32)
        * factor
    )
    places = offset + lax.broadcasted_iota(jnp.int32, (1, 1, cache_block.shape[1]), 2)
    visible = places < limits[:, :, None]
    scores = jnp.where(visible[:, :, None, :], raw_score, NEGATIVE)
    maxima = jnp.max(scores, axis=-1)
    powers = jnp.exp(scores - maxima[..., None])
    totals = jnp.sum(powers, axis=-1)
    weights = powers.astype(jnp.bfloat16)
    summed = jnp.einsum(
        "bqhp,bpd->bqhd",
        weights,
        cache_block[:, :, :latent_width],
        preferred_element_type=jnp.float32,
    )
    return (maxima, totals, (summed / totals[..., None]).astype(jnp.bfloat16))


def merge_sources(partials, maxima, totals):
    highest = jnp.max(maxima, axis=0)
    shares = totals * jnp.exp(maxima - highest[None])
    summed = jnp.sum(shares, axis=0)
    numerator = jnp.sum(shares[..., None] * partials.astype(jnp.float32), axis=0)
    return (highest, summed, numerator / summed[..., None])


def merge_tuple(received):
    return merge_sources(received[0], received[1], received[2])


def join_pairs(earlier, later):
    highest = jnp.maximum(earlier[0], later[0])
    left_share = earlier[1] * jnp.exp(earlier[0] - highest)
    right_share = later[1] * jnp.exp(later[0] - highest)
    summed = left_share + right_share
    blended = (left_share[..., None] * earlier[2] + right_share[..., None] * later[2]) / summed[
        ..., None
    ]
    return (highest, summed, blended)


def absorb(query_nope, query_rope, key_weight):
    absorbed = jnp.einsum(
        "bqhn,hnd->bqhd", query_nope, key_weight, preferred_element_type=jnp.float32
    )
    return jnp.concatenate([absorbed.astype(jnp.bfloat16), query_rope], axis=-1)


def up_project(latent_out, value_weight):
    values = jnp.einsum(
        "bqhd,hde->bqhe", latent_out, value_weight, preferred_element_type=jnp.float32
    ).astype(jnp.bfloat16)
    return values.reshape(values.shape[0], values.shape[1], values.shape[2] * values.shape[3])


def shards(query_nope, query_rope, latent_cache, lengths, key_weight, value_weight, output_weight):
    latent_width = key_weight.shape[2]
    factor = float(query_nope.shape[3] + query_rope.shape[3]) ** (-0.5)
    positions = latent_cache.shape[1]
    drafts = query_nope.shape[1]
    offset = (lax.axis_index(SEQ) * lax.axis_size("grp") + lax.axis_index("grp")) * positions
    limits = lengths[:, None] - drafts + 1 + lax.broadcasted_iota(jnp.int32, (1, drafts), 1)
    own_queries = absorb(query_nope, query_rope, key_weight)
    maxima, totals, partials = shard_partial(
        whole_of(own_queries, (("seq_0", "seq_1"), "seq_2"), 2),
        latent_cache,
        limits,
        offset,
        factor,
        latent_width,
    )
    partials, maxima, totals = (partials, maxima, totals)
    sources = (partials[None], maxima[None], totals[None])
    gathered = merge_tuple(
        (
            lax.all_to_all(
                sources[0].astype(jnp.float32), SEQ, split_axis=3, concat_axis=0, tiled=True
            ).astype(jnp.bfloat16),
            lax.all_to_all(sources[1], SEQ, split_axis=3, concat_axis=0, tiled=True),
            lax.all_to_all(sources[2], SEQ, split_axis=3, concat_axis=0, tiled=True),
        )
    )
    highest, summed, blended = merged((gathered[0], gathered[1], gathered[2]), "grp", join_pairs)
    values = up_project(blended.astype(jnp.bfloat16), value_weight)
    head_terms = jnp.dot(values, output_weight, preferred_element_type=jnp.float32)
    reduced = sum_by_axis(head_terms, (("seq_0", "seq_1"), "seq_2"), 2)
    return reduced.astype(jnp.bfloat16)


def solution(mesh):
    split = Mesh(
        mesh.devices.reshape(16, 4, 2, mesh.shape["grp"]), ("seq_0", "seq_1", "seq_2", "grp")
    )
    in_specs = (
        P(None, None, SEQ, None),
        P(None, None, SEQ, None),
        P(None, SEQ_GRP, None),
        P(),
        P(SEQ, None, None),
        P(SEQ, None, None),
        P(SEQ, "grp"),
    )
    out_specs = P(None, None, GRP_SEQ)
    return jax.shard_map(
        shards, mesh=split, in_specs=in_specs, out_specs=out_specs, check_vma=False
    )
```

profile of v0, /device:TPU:1, one launch (start us, length us, event | category | flops | bytes accessed | tf_op | source)
XLA Modules:
  0.0 228.2 jit_solution(5225242306665096214)
XLA Ops:
  0.0 0.7 copy.149
  0.7 1.0 fusion.6
  1.8 1.2 broadcast_in_dim.28
  3.0 19.3 %all-to-all-start = ((bf16[64,4,2,1,576]{4,2,1,3,0:T(2,128)(2,1)}), bf16[64,4,2,1,576]{4,2,1,3,0:T(2,128)(2,1)S(1)}, u32[]{:S(2)}, u32[]{:S(2)}) async-start(bf16[64,4,2,1,576]{4,2,1,3,0:T(2,128)(2,1)} %broadcast_in_dim.28), calls=%async_computation | async-start | bytes 1310720 | tf_op jit(solution)/shard_map/all_to_all | solution.py:17
  22.5 35.2 %all-to-all-done = bf16[64,4,2,1,576]{4,2,1,3,0:T(2,128)(2,1)S(1)} async-done(((bf16[64,4,2,1,576]{4,2,1,3,0:T(2,128)(2,1)}), bf16[64,4,2,1,576]{4,2,1,3,0:T(2,128)(2,1)S(1)}, u32[]{:S(2)}, u32[]{:S(2)}) %all-to-all-start) | async-done | bytes 589856 | tf_op jit(solution)/shard_map/all_to_all | solution.py:17
  57.6 0.7 broadcast_in_dim.30
  58.3 8.4 %all_to_all.76 = bf16[2,64,4,2,1,576]{5,3,2,1,4,0:T(2,128)(2,1)S(1)} all-to-all(bf16[2,64,4,2,1,576]{5,3,2,1,4,0:T(2,128)(2,1)S(1)} %broadcast_in_dim.30), channel_id=1, replica_groups=mesh['seq_0'=16,'seq_1'=4,'seq_2'=2,'grp'=4] {'seq_2'}, dimensions={0} | all-to-all | bytes 2359296 | tf_op jit(solution)/shard_map/all_to_all | solution.py:17
  66.8 0.9 copy.151
  67.7 2.1 copy.152
  69.8 2.1 fusion.42
  71.8 0.4 fusion.11
  72.2 0.8 copy.153
  73.0 6.5 %all-to-all-start.2 = ((f32[1,4,2,128]{1,2,0,3:T(2,128)}), f32[1,4,2,128]{1,2,0,3:T(2,128)S(1)}, u32[]{:S(2)}, u32[]{:S(2)}) async-start(f32[1,4,2,128]{1,2,0,3:T(2,128)} %copy.153), calls=%async_computation.2 | async-start | bytes 262144 | tf_op jit(solution)/shard_map/all_to_all | solution.py:165
  79.6 0.8 copy.154
  80.4 15.2 %all-to-all-done.2 = f32[1,4,2,128]{1,2,0,3:T(2,128)S(1)} async-done(((f32[1,4,2,128]{1,2,0,3:T(2,128)}), f32[1,4,2,128]{1,2,0,3:T(2,128)S(1)}, u32[]{:S(2)}, u32[]{:S(2)}) %all-to-all-start.2) | async-done | bytes 4128 | tf_op jit(solution)/shard_map/all_to_all | solution.py:165
  95.6 7.2 %all-to-all-start.3 = ((f32[1,4,2,128]{1,2,0,3:T(2,128)}), f32[1,4,2,128]{1,2,0,3:T(2,128)S(1)}, u32[]{:S(2)}, u32[]{:S(2)}) async-start(f32[1,4,2,128]{1,2,0,3:T(2,128)} %copy.154), calls=%async_computation.3 | async-start | bytes 262144 | tf_op jit(solution)/shard_map/all_to_all | solution.py:164
  102.8 0.5 fusion.2
  103.3 2.1 copy.157
  105.4 13.4 %all-to-all-done.3 = f32[1,4,2,128]{1,2,0,3:T(2,128)S(1)} async-done(((f32[1,4,2,128]{1,2,0,3:T(2,128)}), f32[1,4,2,128]{1,2,0,3:T(2,128)S(1)}, u32[]{:S(2)}, u32[]{:S(2)}) %all-to-all-start.3) | async-done | bytes 4128 | tf_op jit(solution)/shard_map/all_to_all | solution.py:164
  118.7 7.2 %all-to-all-start.4 = ((bf16[1,4,2,128,512]{4,2,1,0,3:T(2,128)(2,1)}), bf16[1,4,2,128,512]{4,2,1,0,3:T(2,128)(2,1)S(1)}, u32[]{:S(2)}, u32[]{:S(2)}) async-start(bf16[1,4,2,128,512]{4,2,1,0,3:T(2,128)(2,1)} %copy.157), calls=%async_computation.4 | async-start | bytes 2097152 | tf_op jit(solution)/shard_map/all_to_all | solution.py:161
  126.3 0.9 copy.155
  127.7 50.4 %all-to-all-done.4 = bf16[1,4,2,128,512]{4,2,1,0,3:T(2,128)(2,1)S(1)} async-done(((bf16[1,4,2,128,512]{4,2,1,0,3:T(2,128)(2,1)}), bf16[1,4,2,128,512]{4,2,1,0,3:T(2,128)(2,1)S(1)}, u32[]{:S(2)}, u32[]{:S(2)}) %all-to-all-start.4) | async-done | bytes 1048608 | tf_op jit(solution)/shard_map/all_to_all | solution.py:161
  178.1 1.2 fusion
  179.4 0.6 broadcast_in_dim.34
  180.0 4.0 %all-to-all-start.5 = ((f32[4,10,512]{2,1,0:T(8,128)}), f32[4,10,512]{2,1,0:T(8,128)S(1)}, u32[]{:S(2)}, u32[]{:S(2)}) async-start(f32[4,10,512]{2,1,0:T(8,128)} %broadcast_in_dim.34), calls=%async_computation.5 | async-start | bytes 262144 | tf_op jit(solution)/shard_map/all_to_all | solution.py:17
  184.4 4.5 %all-to-all-done.5 = f32[4,10,512]{2,1,0:T(8,128)S(1)} async-done(((f32[4,10,512]{2,1,0:T(8,128)}), f32[4,10,512]{2,1,0:T(8,128)S(1)}, u32[]{:S(2)}, u32[]{:S(2)}) %all-to-all-start.5) | async-done | bytes 81952 | tf_op jit(solution)/shard_map/all_to_all | solution.py:17
  190.9 0.5 fusion.12
  191.6 6.9 %all_to_all.77 = f32[2,1,7168]{2,1,0:T(1,128)S(1)} all-to-all(f32[2,1,7168]{2,1,0:T(1,128)S(1)} %reshape.222), channel_id=1, replica_groups=mesh['seq_0'=16,'seq_1'=4,'seq_2'=2,'grp'=4] {'seq_2'}, dimensions={0} | all-to-all | bytes 114688 | tf_op jit(solution)/shard_map/all_to_all | solution.py:71
  198.5 0.5 broadcast.75
  199.0 0.8 reduce.4
  200.2 27.3 %all_to_all.78 = f32[64,4,2,14]{3,1,2,0:T(4,128)S(1)} all-to-all(f32[64,4,2,14]{3,1,2,0:T(4,128)S(1)} %copy.179), channel_id=1, replica_groups=mesh['seq_0'=16,'seq_1'=4,'seq_2'=2,'grp'=4] {'seq_0','seq_1'}, dimensions={0} | all-to-all | bytes 57344 | tf_op jit(solution)/shard_map/all_to_all | solution.py:79
  227.6 0.6 copy.182
  (60 shorter events, 3.9 us)
Async XLA Ops:
  0.0 190.9 %copy-start = (bf16[1,512,128]{2,1,0:T(8,128)(2,1)S(1)}, bf16[1,512,128]{2,1,0:T(8,128)(2,1)}, u32[]{:S(2)}) copy-start(bf16[1,512,128]{2,1,0:T(8,128)(2,1)} %param.12) | copy-start | bytes 393220
  0.0 22.3 %copy-start.3 = (s32[4]{0:T(128)S(1)}, s32[4]{0:T(128)}, u32[]{:S(2)}) copy-start(s32[4]{0:T(128)} %param.10) | copy-start | bytes 52
  3.0 54.6 %all-to-all-start = ((bf16[64,4,2,1,576]{4,2,1,3,0:T(2,128)(2,1)}), bf16[64,4,2,1,576]{4,2,1,3,0:T(2,128)(2,1)S(1)}, u32[]{:S(2)}, u32[]{:S(2)}) async-start(bf16[64,4,2,1,576]{4,2,1,3,0:T(2,128)(2,1)} %broadcast_in_dim.28), calls=%async_computation | async-start | bytes 1310720 | tf_op jit(solution)/shard_map/all_to_all | solution.py:17
  71.8 30.9 %copy-start.2 = (bf16[4,256,576]{1,2,0:T(8,128)(2,1)S(1)}, bf16[4,256,576]{1,2,0:T(8,128)(2,1)}, u32[]{:S(2)}) copy-start(bf16[4,256,576]{1,2,0:T(8,128)(2,1)} %param.9) | copy-start | bytes 3538948
  73.0 22.5 %all-to-all-start.2 = ((f32[1,4,2,128]{1,2,0,3:T(2,128)}), f32[1,4,2,128]{1,2,0,3:T(2,128)S(1)}, u32[]{:S(2)}, u32[]{:S(2)}) async-start(f32[1,4,2,128]{1,2,0,3:T(2,128)} %copy.153), calls=%async_computation.2 | async-start | bytes 262144 | tf_op jit(solution)/shard_map/all_to_all | solution.py:165
  95.6 23.2 %all-to-all-start.3 = ((f32[1,4,2,128]{1,2,0,3:T(2,128)}), f32[1,4,2,128]{1,2,0,3:T(2,128)S(1)}, u32[]{:S(2)}, u32[]{:S(2)}) async-start(f32[1,4,2,128]{1,2,0,3:T(2,128)} %copy.154), calls=%async_computation.3 | async-start | bytes 262144 | tf_op jit(solution)/shard_map/all_to_all | solution.py:164
  118.7 59.3 %all-to-all-start.4 = ((bf16[1,4,2,128,512]{4,2,1,0,3:T(2,128)(2,1)}), bf16[1,4,2,128,512]{4,2,1,0,3:T(2,128)(2,1)S(1)}, u32[]{:S(2)}, u32[]{:S(2)}) async-start(bf16[1,4,2,128,512]{4,2,1,0,3:T(2,128)(2,1)} %copy.157), calls=%async_computation.4 | async-start | bytes 2097152 | tf_op jit(solution)/shard_map/all_to_all | solution.py:161
  126.3 57.7 %copy-start.1 = (bf16[128,1792]{1,0:T(8,128)(2,1)S(1)}, bf16[128,1792]{1,0:T(8,128)(2,1)}, u32[]{:S(2)}) copy-start(bf16[128,1792]{1,0:T(8,128)(2,1)} %param.13) | copy-start | bytes 1376260
  180.0 8.8 %all-to-all-start.5 = ((f32[4,10,512]{2,1,0:T(8,128)}), f32[4,10,512]{2,1,0:T(8,128)S(1)}, u32[]{:S(2)}, u32[]{:S(2)}) async-start(f32[4,10,512]{2,1,0:T(8,128)} %broadcast_in_dim.34), calls=%async_computation.5 | async-start | bytes 262144 | tf_op jit(solution)/shard_map/all_to_all | solution.py:17
where the time goes:
time: 230 us; the launch traced here: 228 us
  waiting for transfers between devices  119 us (52%)
  starting transfers between devices  44.2 us (19%)
  blocking collectives  42.7 us (19%)
  local copies, waits for them, and re-layouts  14.8 us (6%)
  matrix products  4.14 us (2%)
  other arithmetic  3.4 us (1%)
    all_to_all x1, waiting for transfers between devices, shards(): lax.all_to_all(sources[0].astype(jnp.float32), SEQ, split_axis=3, concat_...  50.4 us
    all_to_all x2, waiting for transfers between devices, from_everyone(): lax.all_to_all(jnp.broadcast_to(array[None], (devices, *array.shape)), ax...  39.7 us
    all_to_all x1, blocking collectives, sum_by_axis(): lax.all_to_all(nearer, far, split_axis=0, concat_axis=0, tiled=True)  27.3 us
    all_to_all x2, starting transfers between devices, from_everyone(): lax.all_to_all(jnp.broadcast_to(array[None], (devices, *array.shape)), ax...  23.3 us
    all_to_all x1, waiting for transfers between devices, shards(): lax.all_to_all(sources[2], SEQ, split_axis=3, concat_axis=0, tiled=True)  15.2 us
    all_to_all x1, waiting for transfers between devices, shards(): lax.all_to_all(sources[1], SEQ, split_axis=3, concat_axis=0, tiled=True)  13.4 us
    all_to_all x1, blocking collectives, from_everyone(): lax.all_to_all(jnp.broadcast_to(array[None], (devices, *array.shape)), ax...  8.43 us
    all_to_all x1, starting transfers between devices, shards(): lax.all_to_all(sources[0].astype(jnp.float32), SEQ, split_axis=3, concat_...  7.22 us
  transfers between devices with their start and end apart: 5, of which 5 were waited for; matrix products, arithmetic and copies ran while one was open for 2% of the time, Pallas kernels for 0%

commit v1 on v0

v1 whole, which is shorter than its diff:
```python
import functools

import jax
import jax.numpy as jnp
from jax import lax
from jax.experimental import pallas as pl
from jax.experimental.pallas import tpu as pltpu
from jax.sharding import Mesh
from jax.sharding import PartitionSpec as P

SEQ = ("z", "y", "c")
SEQ_GRP = ("z", "y", "c", "x")
GRP_SEQ = ("x", "z", "y", "c")
MESH = pl.DeviceIdType.MESH
NEGATIVE = -1e30
F32, BF16 = jnp.float32, jnp.bfloat16


def ring_offsets(n):
    order = [0]
    for d in range(1, n // 2):
        order += [d, -d]
    return order + [n // 2] if n > 1 else order


def by_distance(n):
    return sorted(range(n), key=lambda d: (-min(d, n - d), d))


def kernel(
    dims, factor,
    qn_hbm, qr_hbm, kv_hbm, len_hbm, kw_hbm, vw_hbm, ow_hbm,
    out_ref,
    qn, qr, lens, kw, vw, ow, kv,
    qz, qf, qall,
    osend, orecv, ssend, srecv,
    zf, zsend, zrecv,
    vx, vf,
    czsend, czrecv, cysend, cyrecv,
    local_sem, kv_sem, z_sem, xy_sem, o_sem, s_sem, b_sem, v_sem, cz_sem, cy_sem,
):
    nz, ny, nc, nx = dims
    z, y, c, x = (lax.axis_index(a) for a in SEQ_GRP)
    offs = ring_offsets(nz)
    half = nz // 2
    dl = kw.shape[1]
    ctx = kv.shape[2]
    rows = 2 * nz * ny
    wide = 2 * half
    plane = [(dx, dy) for dx in by_distance(nx) for dy in by_distance(ny) if (dx, dy) != (0, 0)]

    def near(v, d, n):
        return lax.rem(v + (d % n), n)

    barrier = pltpu.get_barrier_semaphore()
    peers = 0
    for k in range(nz - 1, 0, -1):
        pl.semaphore_signal(barrier, inc=1, device_id={"z": near(z, offs[k], nz)}, device_id_type=MESH)
        peers += 1
    for dx, dy in plane:
        pl.semaphore_signal(
            barrier, inc=1, device_id={"x": near(x, dx, nx), "y": near(y, dy, ny)}, device_id_type=MESH
        )
        peers += 1
    for dy in range(ny):
        pl.semaphore_signal(
            barrier, inc=1, device_id={"y": near(y, dy, ny), "c": 1 - c}, device_id_type=MESH
        )
        peers += 1

    loads = [
        pltpu.make_async_copy(src, dst, local_sem.at[i])
        for i, (src, dst) in enumerate(
            [
                (qn_hbm, qn), (qr_hbm, qr), (kw_hbm.at[0], kw), (kv_hbm, kv.at[c]),
                (len_hbm, lens), (vw_hbm.at[0], vw), (ow_hbm, ow),
            ]
        )
    ]
    for load in loads:
        load.start()

    for i in (0, 1, 2):
        loads[i].wait()
    absorbed = jnp.dot(qn[x], kw[...], preferred_element_type=F32)
    qz[0, :, :dl] = absorbed.astype(BF16)
    qz[0, :, dl:] = qr[x]

    pl.semaphore_wait(barrier, peers)

    started = []

    def send(src, dst, sems, at, device):
        copy = pltpu.make_async_remote_copy(
            src_ref=src, dst_ref=dst, send_sem=sems.at[(0, *at)], recv_sem=sems.at[(1, *at)],
            device_id=device, device_id_type=MESH,
        )
        copy.start()
        started.append(copy)
        return copy

    zcopies = {}
    for k in range(nz - 1, 0, -1):
        zcopies[k] = send(qz.at[0], qz.at[k], z_sem, (k,), {"z": near(z, -offs[k], nz)})
    kvcopy = send(kv_hbm, kv.at[c], kv_sem, (0,), {"c": 1 - c})

    xycopies = []
    for g in range(2):
        for i in range(half):
            k = g * half + i
            if k:
                zcopies[k].wait_recv()
            qf[2 * i : 2 * i + 2, :] = qz[k].astype(F32)
        qall[x, g, y] = qf[...].astype(BF16)
        for dx, dy in plane:
            xycopies.append(
                send(
                    qall.at[x, g, y], qall.at[x, g, y], xy_sem, (g, dx * ny + dy),
                    {"x": near(x, dx, nx), "y": near(y, dy, ny)},
                )
            )

    for i in (3, 4):
        loads[i].wait()
    kvcopy.wait_recv()
    for copy in xycopies:
        copy.wait_recv()

    row = lax.broadcasted_iota(jnp.int32, (rows, ctx), 0)
    place = lax.broadcasted_iota(jnp.int32, (rows, ctx), 1)
    drafts = lax.rem(row, 2)
    eye = lax.broadcasted_iota(jnp.int32, (rows, rows), 0) == lax.broadcasted_iota(
        jnp.int32, (rows, rows), 1
    )
    ocopies, scopies = {}, {}
    for dx in by_distance(nx):
        b = near(x, dx, nx)
        q = qall[b].reshape(rows, qall.shape[-1])
        limit = lens[b] - 1 + drafts
        scores, seen = [], []
        for e in range(nc):
            start = (((z * ny + y) * nc + e) * nx + x) * ctx
            raw = lax.dot_general(
                q, kv[e, b], (((1,), (1,)), ((), ())), preferred_element_type=F32
            ) * factor
            seen.append(place + start < limit)
            scores.append(jnp.where(seen[e], raw, NEGATIVE))
        top = functools.reduce(jnp.maximum, [jnp.max(s, axis=1, keepdims=True) for s in scores])
        expo = [jnp.where(m, jnp.exp(s - top), 0.0) for m, s in zip(seen, scores)]
        total = sum(jnp.sum(e, axis=1, keepdims=True) for e in expo)
        numer = sum(
            jnp.dot(expo[e].astype(BF16), kv[e, b, :, :dl], preferred_element_type=F32)
            for e in range(nc)
        )
        blocks = numer.astype(BF16).reshape(2, ny, wide, dl)
        for g in range(2):
            osend[b, :, g] = blocks[g]
        ssend[b, 0:1, :] = jnp.sum(jnp.where(eye, top, 0.0), axis=0, keepdims=True)
        ssend[b, 1:2, :] = jnp.sum(jnp.where(eye, total, 0.0), axis=0, keepdims=True)
        for dy in by_distance(ny):
            if (dx, dy) == (0, 0):
                continue
            device = {"x": b, "y": near(y, dy, ny)}
            j = dx * ny + dy
            scopies[j] = send(ssend.at[b], srecv.at[j], s_sem, (j,), device)
            ocopies[j] = send(osend.at[b, near(y, dy, ny)], orecv.at[j], o_sem, (j,), device)

    order = [0] + [dx * ny + dy for dx, dy in reversed(plane)]
    for j in order[1:]:
        scopies[j].wait_recv()
    stats = {j: (ssend[x] if j == 0 else srecv[j]) for j in order}
    peak = functools.reduce(jnp.maximum, [stats[j][0:1] for j in order])
    peak_hi = peak.astype(BF16).astype(F32)
    peak_lo = (peak - peak_hi).astype(BF16).astype(F32)
    level = peak_hi + peak_lo
    scale = {j: jnp.exp(jnp.minimum(stats[j][0:1] - level, 16.0)) for j in order}
    denom = sum(scale[j] * stats[j][1:2] for j in order)
    denom_hi = denom.astype(BF16).astype(F32)
    denom_lo = (denom - denom_hi).astype(BF16).astype(F32)

    own = lax.broadcasted_iota(jnp.int32, (2 * wide, rows), 0)
    own = lax.div(own, wide) * (ny * wide) + y * wide + lax.rem(own, wide)
    pick = own == lax.broadcasted_iota(jnp.int32, (2 * wide, rows), 1)

    def column(values):
        return jnp.sum(jnp.where(pick, values, 0.0), axis=1, keepdims=True)

    merged = None
    for j in order:
        if j:
            ocopies[j].wait_recv()
        block = osend[x, y] if j == 0 else orecv[j]
        term = column(scale[j]) * block.reshape(2 * wide, dl).astype(F32)
        merged = term if merged is None else merged + term
    zf[:, :dl] = merged
    lane = lax.broadcasted_iota(jnp.int32, (2 * wide, 128), 1)
    zf[:, dl:] = jnp.where(
        lane < 64,
        jnp.where(lane < 32, column(peak_hi), column(peak_lo)),
        jnp.where(lane < 96, column(denom_hi), column(denom_lo)),
    )
    for k in range(nz):
        zsend[k] = zf[2 * k : 2 * k + 2, :].astype(BF16)

    bcopies = {}
    for k in range(nz - 1, 0, -1):
        bcopies[k] = send(zsend.at[k], zrecv.at[k], b_sem, (k,), {"z": near(z, offs[k], nz)})
    for i in (5, 6):
        loads[i].wait()
    parts = []
    for k in range(nz):
        if k:
            bcopies[k].wait_recv()
        parts.append((zrecv[k] if k else zsend[0]).astype(F32))
    tops = [p[:, dl : dl + 1] + p[:, dl + 32 : dl + 33] for p in parts]
    sums = [p[:, dl + 64 : dl + 65] + p[:, dl + 96 : dl + 97] for p in parts]
    highest = functools.reduce(jnp.maximum, tops)
    shares = [jnp.exp(t - highest) for t in tops]
    bottom = sum(s * t for s, t in zip(shares, sums))
    latent = sum(s * p[:, :dl] for s, p in zip(shares, parts)) / bottom
    values = jnp.dot(latent.astype(BF16), vw[...], preferred_element_type=F32)
    vx[x] = values.astype(BF16)

    vcopies = [
        send(vx.at[x], vx.at[x], v_sem, (dx,), {"x": near(x, dx, nx)})
        for dx in by_distance(nx)
        if dx
    ]
    for copy in vcopies:
        copy.wait_recv()
    for b in range(nx):
        vf[2 * b : 2 * b + 2, :] = vx[b].astype(F32)
    terms = jnp.dot(vf[...].astype(BF16), ow[...], preferred_element_type=F32)

    cols = czsend.shape[2]
    for j in range(nz):
        czsend[j] = terms[:, j * cols : (j + 1) * cols].astype(BF16)
    czcopies = {}
    for k in range(nz - 1, 0, -1):
        dest = near(z, offs[k], nz)
        czcopies[k] = send(czsend.at[dest], czrecv.at[k], cz_sem, (k,), {"z": dest})
    summed = czsend[z].astype(F32)
    for k in range(1, nz):
        czcopies[k].wait_recv()
        summed = summed + czrecv[k].astype(F32)
    cysend[...] = summed
    cycopies = {}
    for dy in by_distance(ny):
        for dc in range(nc - 1, -1, -1):
            if (dy, dc) == (0, 0):
                continue
            j = dy * nc + dc
            cycopies[j] = send(
                cysend, cyrecv.at[j], cy_sem, (j,),
                {"y": near(y, dy, ny), "c": near(c, dc, nc)},
            )
    for j in range(1, ny * nc):
        cycopies[j].wait_recv()
        summed = summed + cyrecv[j]
    width = cols // (ny * nc)
    mine = y * nc + c
    result = summed[:, :width]
    for j in range(1, ny * nc):
        result = jnp.where(mine == j, summed[:, j * width : (j + 1) * width], result)
    out_ref[...] = result.astype(BF16)

    for copy in started:
        copy.wait_send()


def shards(dims, query_nope, query_rope, latent_cache, lengths, key_weight, value_weight, output_weight):
    nz, ny, nc, nx = dims
    dn, dr = query_nope.shape[3], query_rope.shape[3]
    dl, dv = key_weight.shape[2], value_weight.shape[2]
    nb, ctx, dk = latent_cache.shape
    dm = output_weight.shape[1]
    assert nb == nx and query_nope.shape[1] == 2 and query_nope.shape[2] == 1
    half = nz // 2
    wide = 2 * half
    rows = 2 * nz * ny
    cols = dm // nz
    factor = float(dn + dr) ** (-0.5)
    dma = pltpu.SemaphoreType.DMA
    hbm = pl.BlockSpec(memory_space=pl.ANY)
    result = pl.pallas_call(
        functools.partial(kernel, dims, factor),
        out_shape=jax.ShapeDtypeStruct((2 * nb, cols // (ny * nc)), BF16),
        in_specs=[hbm] * 7,
        out_specs=pl.BlockSpec(memory_space=pltpu.VMEM),
        scratch_shapes=[
            pltpu.VMEM((nb, 2, dn), BF16),
            pltpu.VMEM((nb, 2, dr), BF16),
            pltpu.SMEM((nb,), jnp.int32),
            pltpu.VMEM((dn, dl), BF16),
            pltpu.VMEM((dl, dv), BF16),
            pltpu.VMEM((dv, dm), BF16),
            pltpu.VMEM((nc, nb, ctx, dk), BF16),
            pltpu.VMEM((nz, 2, dk), BF16),
            pltpu.VMEM((wide, dk), F32),
            pltpu.VMEM((nb, 2, ny, wide, dk), BF16),
            pltpu.VMEM((nb, ny, 2, wide, dl), BF16),
            pltpu.VMEM((nx * ny, 2, wide, dl), BF16),
            pltpu.VMEM((nb, 2, rows), F32),
            pltpu.VMEM((nx * ny, 2, rows), F32),
            pltpu.VMEM((2 * wide, dl + 128), F32),
            pltpu.VMEM((nz, 2, dl + 128), BF16),
            pltpu.VMEM((nz, 2, dl + 128), BF16),
            pltpu.VMEM((nb, 2, dv), BF16),
            pltpu.VMEM((2 * nb, dv), F32),
            pltpu.VMEM((nz, 2 * nb, cols), BF16),
            pltpu.VMEM((nz, 2 * nb, cols), BF16),
            pltpu.VMEM((2 * nb, cols), F32),
            pltpu.VMEM((ny * nc, 2 * nb, cols), F32),
            dma((7,)),
            dma((2, 1)),
            dma((2, nz)),
            dma((2, 2, nx * ny)),
            dma((2, nx * ny)),
            dma((2, nx * ny)),
            dma((2, nz)),
            dma((2, nx)),
            dma((2, nz)),
            dma((2, ny * nc)),
        ],
        compiler_params=pltpu.CompilerParams(collective_id=0, has_side_effects=True),
    )(
        query_nope.reshape(nb, 2, dn),
        query_rope.reshape(nb, 2, dr),
        latent_cache,
        lengths,
        key_weight,
        value_weight,
        output_weight,
    )
    return result.reshape(nb, 2, -1)


def solution_dims(mesh, dims):
    split = Mesh(mesh.devices.reshape(dims), SEQ_GRP)
    in_specs = (
        P(None, None, SEQ, None),
        P(None, None, SEQ, None),
        P(None, SEQ_GRP, None),
        P(),
        P(SEQ, None, None),
        P(SEQ, None, None),
        P(SEQ, "x"),
    )
    return jax.shard_map(
        functools.partial(shards, dims),
        mesh=split,
        in_specs=in_specs,
        out_specs=P(None, None, GRP_SEQ),
        check_vma=False,
    )


def solution(mesh):
    ny, nc = 4, 2
    nz = mesh.shape["seq"] // (ny * nc)
    return solution_dims(mesh, (nz, ny, nc, mesh.shape["grp"]))
```

time: 230 us -> 68.6 us (0.30)
  waiting for transfers between devices: 119 us -> 0 us
  Pallas kernels: 0 us -> 64.7 us
  starting transfers between devices: 44.2 us -> 0 us
  blocking collectives: 42.7 us -> 0 us
  local copies, waits for them, and re-layouts: 14.8 us -> 3.66 us
  matrix products: 4.14 us -> 0 us
  other arithmetic: 3.4 us -> 0 us
    all_to_all x5 -> x0, waiting for transfers between devices: 119 us -> none  [the longest x1 50.4 us: shards(): lax.all_to_all(sources[0].astype(jnp.float32), SEQ, split_axis=3, concat_...]
    pallas_call x0 -> x1, Pallas kernels: none -> 64.7 us  [shards(): pl.pallas_call(functools.partial(kernel, dims, factor), out_shape=jax.Sha...]
    all_to_all x5 -> x0, starting transfers between devices: 44.2 us -> none  [the longest x2 23.3 us: from_everyone(): lax.all_to_all(jnp.broadcast_to(array[None], (devices, *array.shape)), ax...]
    all_to_all x3 -> x0, blocking collectives: 42.7 us -> none  [the longest x1 27.3 us: sum_by_axis(): lax.all_to_all(nearer, far, split_axis=0, concat_axis=0, tiled=True)]
    dot_general x4 -> x0, matrix products: 4.14 us -> none  [the longest x1 2.06 us: shard_partial(): jnp.einsum('bqhd,bpd->bqhp', queries, cache_block, preferred_element_type...]
    broadcast_in_dim x6 -> x0, local copies, waits for them, and re-layouts: 4.09 us -> none  [the longest x4 2.51 us: from_everyone(): jnp.broadcast_to(array[None], (devices, *array.shape))]
    convert_element_type x2 -> x0, local copies, waits for them, and re-layouts: 2.65 us -> none  [the longest x1 2.07 us: shards(): sources[0].astype(jnp.float32)]
  transfers between devices with their start and end apart: 5 -> 0, of which waited for: 5 -> 0; matrix products, arithmetic and copies ran while one was open for 2% -> 0% of each run, Pallas kernels for 0% -> 0%
where the time goes in v1:
time: 68.6 us; the launch traced here: 68.4 us
  Pallas kernels  64.7 us (94%)
  local copies, waits for them, and re-layouts  3.66 us (5%)
    pallas_call x1, Pallas kernels, shards(): pl.pallas_call(functools.partial(kernel, dims, factor), out_shape=jax.Sha...  64.7 us
    unnamed x2, local copies, waits for them, and re-layouts  3.66 us

profile of v1, /device:TPU:1, one launch (start us, length us, event | category | flops | bytes accessed | tf_op | source)
XLA Modules:
  0.0 68.4 jit_solution(16130687927418078000)
XLA Ops:
  0.0 2.4 %copy.8.kv_hbm = bf16[4,256,576]{2,1,0:T(8,128)(2,1)} copy(bf16[4,256,576]{1,2,0:T(8,128)(2,1)} %param.9) | data formatting | bytes 2359296 | tf_op args[2]
  2.4 64.7 %shard_map.73 = bf16[8,14]{1,0:T(8,128)(2,1)} custom-call(bf16[4,2,128]{2,1,0:T(2,128)(2,1)} %bitcast.4, bf16[4,2,64]{2,1,0:T(2,128)(2,1)} %bitcast.5, bf16[4,256,576]{2,1,0:T(8,128)(2,1)} %copy.8.kv_hbm, s32[4]{0:T(128)} %len_hbm.1, bf16[1,128,512]{2,1,0:T(8,128)(2,1)} %kw_hbm.1, bf16[1,512,128]{2,1,0:T(8,128)(2,1)} %vw_hbm.1, bf16[128,1792]{1,0:T(8,128)(2,1)} %ow_hbm.1), custom_call_target="tpu_custom_call" | custom-call | tf_op jit(solution)/shard_map/pallas_call | solution.py:285
  67.1 1.2 %copy.10 = bf16[4,2,14]{2,1,0:T(2,128)(2,1)} copy(bf16[4,2,14]{2,1,0:T(2,128)(2,1)} %bitcast.3) | data formatting | bytes 448
